TPU v7x, 128 devices: a whole 4x4x4 slice. The times are simulated.
128 devices in a mesh: dp: 8 (over y, core), tensor: 16 (over x, z).
Axes of the slice: x: 4, y: 4, z: 4, core: 2. Of those that a mesh axis runs over, the one named last changes fastest.
Arguments:
- ref_hidden: bfloat16 [2304, 4608], P('dp', 'tensor'), may hold values from -6 to 6
- pol_hidden: bfloat16 [2304, 4608], P('dp', 'tensor'), may hold values from -6 to 6
- readout: bfloat16 [2304, 4608], P('dp', 'tensor'), may hold values from -0.019897461 to 0.019897461
- lengths: int32 [24], P('dp'), may hold values from 16 to 96, as said below
- pairing: int32 [24], replicated, may hold values from 0 to 23, each once
- pre_gain: float32 [4608], replicated, may hold values from 0.25 to 1.75
- post_gain: float32 [4608], replicated, may hold values from 0.25 to 1.75
- w_query: bfloat16 [4608, 4096], P('dp', 'tensor'), may hold values from -0.09375 to 0.09375
- w_key: bfloat16 [4608, 2048], P('dp', 'tensor'), may hold values from -3 to 3
- value_projection: bfloat16 [4608, 2048], P('dp', 'tensor'), may hold values from -0.09375 to 0.09375
- w_out: bfloat16 [4608, 4096], P('dp', 'tensor'), may hold values from -0.09375 to 0.09375
- a_query: bfloat16 [4608, 64], P('dp'), may hold values from -0.09375 to 0.09375
- a_value: bfloat16 [4608, 64], P('dp'), may hold values from -0.09375 to 0.09375
- query_second_factor: bfloat16 [64, 4096], P(None, 'tensor'), may hold values from -0.75 to 0.75
- value_second_factor: bfloat16 [64, 2048], P(None, 'tensor'), may hold values from -0.75 to 0.75
Outputs:
- policy_out: bfloat16 [2304, 4608], P('dp', 'tensor')
- reference_out: bfloat16 [2304, 4608], P('dp', 'tensor')
- dpo_loss: float32 [], replicated
- grad_hidden: bfloat16 [2304, 4608], P('dp', 'tensor')
- grad_a: float32 [4608, 128], P('dp')
- query_factor_gradient: float32 [64, 4096], P(None, 'tensor')
- value_factor_gradient: float32 [64, 2048], P(None, 'tensor')
Inputs may be any that keep to these rules, and one draw needn't show every extreme that they name: `lengths`: every sequence has at least one valid token and some sequence is full. `pairing`: entries 2k and 2k + 1 name the chosen and the rejected sequence of pair k; every sequence appears once.
All inputs are finite; a program needn't handle non-finite values.
Results may differ from a plain program's by a relative error of at most 0.0233.
The roundings to bfloat16 on the way count: a program that leaves them out, or rounds other values in their place, can miss the bound.
Values may be sent and summed in bfloat16 or wider, within the bound.
A program may use at most 128 MiB of HBM per device.

v0:
```python
import functools
import jax
import jax.numpy as jnp
from jax import lax
from jax.sharding import Mesh
from jax.sharding import PartitionSpec as P

MODEL_WIDTH = 4608
HQ = 32
HEAD_SIZE = 128
TENSOR = ("tensor_0", "tensor_1")
DP = ("dp_0", "dp_1")
DP_TENSOR = ("dp_0", "dp_1", "tensor_0", "tensor_1")
NORM_EPS = 1e-06
SOFT_CAP = 50.0
ADAPTER_SCALE = 0.5
DPO_BETA = 0.5
LOSS_SCALE = 256.0
ROPE_BASE = 10000.0


def one_axis_at_a_time(shard, axes):
    return functools.reduce(lax.psum, axes, shard)


def copy_for_each(shard, axis):
    count = lax.axis_size(axis)
    return lax.all_to_all(
        jnp.broadcast_to(shard[None], (count, *shard.shape)), axis, 0, 0, tiled=True
    )


def in_order(tiles, dim):
    shape = list(tiles.shape[1:])
    shape[dim] *= tiles.shape[0]
    return jnp.moveaxis(tiles, 0, dim).reshape(shape)


def collect(shard, axis, dim):
    tiles = copy_for_each(shard, axis)
    return in_order(tiles, dim)


def split_up(shard, dim, count):
    shape = shard.shape
    tiles = shard.reshape(*shape[:dim], count, shape[dim] // count, *shape[dim + 1 :])
    return jnp.moveaxis(tiles, dim, 0)


def summed_on_arrival(shard, axis, dim):
    tiles = split_up(shard, dim, lax.axis_size(axis))
    arrived = lax.all_to_all(tiles, axis, split_axis=0, concat_axis=0, tiled=True)
    return arrived.astype(jnp.float32).sum(axis=0)


def sent_together(arrays, axis, dim, along):
    ends, at = ([], 0)
    for a in arrays[:-1]:
        at += a.shape[along]
        ends.append(at)
    both = jnp.concatenate(arrays, axis=along)
    return tuple(jnp.split(lax.all_gather(both, axis, axis=dim, tiled=True), ends, axis=along))


def over_copies(shard, axis):
    return copy_for_each(shard, axis).astype(jnp.float32).sum(axis=0)


def query_scale():
    return float(MODEL_WIDTH // HQ) ** (-0.5)


def apply_rotation(value_rows, direction):
    length = value_rows.shape[1]
    head_depth = value_rows.shape[3]
    middle = head_depth // 2
    spacing = ROPE_BASE ** (-2.0 * jnp.arange(middle, dtype=jnp.float32) / head_depth)
    angles = jnp.arange(length, dtype=jnp.float32)[:, None] * spacing[None, :]
    cosine = jnp.cos(angles)[None, :, None, :]
    sine_part = direction * jnp.sin(angles)[None, :, None, :]
    leading = value_rows[..., :middle]
    trailing = value_rows[..., middle:]
    return jnp.concatenate(
        [leading * cosine - trailing * sine_part, trailing * cosine + leading * sine_part], axis=-1
    )


def allowed_mask(lengths, length):
    places = jnp.arange(length)
    causal = places[None, :] <= places[:, None]
    living = places[None, :] < lengths[:, None]
    return causal[None, None, None, :, :] & living[:, None, None, None, :]


def attend(query_rows, rotated_keys, value_rows, lengths):
    seqs_here, length, q_heads, head_depth = query_rows.shape
    kv_heads = rotated_keys.shape[2]
    grouped_heads = query_rows.reshape(seqs_here, length, kv_heads, q_heads // kv_heads, head_depth)
    scores = (
        jnp.einsum(
            "sqkgd,spkd->skgqp", grouped_heads, rotated_keys, preferred_element_type=jnp.float32
        )
        * query_scale()
    )
    capped = SOFT_CAP * jnp.tanh(scores / SOFT_CAP)
    allowed = allowed_mask(lengths, length)
    weights = jnp.where(allowed, jnp.exp(capped), 0.0)
    probabilities = weights / jnp.sum(weights, axis=-1, keepdims=True)
    probs_low = probabilities.astype(jnp.bfloat16)
    mixed_out = jnp.einsum(
        "skgqp,spkd->sqkgd", probs_low, value_rows, preferred_element_type=jnp.float32
    )
    return (
        mixed_out.astype(jnp.bfloat16).reshape(seqs_here, length, q_heads, head_depth),
        probs_low,
        probabilities,
        capped,
    )


def attend_back(grad_mixed, query_rows, rotated_keys, value_rows, probs_low, probabilities, capped):
    seqs_here, length, q_heads, head_depth = query_rows.shape
    kv_heads = rotated_keys.shape[2]
    shape_five = (seqs_here, length, kv_heads, q_heads // kv_heads, head_depth)
    grouped_heads = query_rows.reshape(shape_five)
    grad_grouped = grad_mixed.reshape(shape_five)
    grad_probs = jnp.einsum(
        "sqkgd,spkd->skgqp", grad_grouped, value_rows, preferred_element_type=jnp.float32
    )
    value_rows_gradient = jnp.einsum(
        "skgqp,sqkgd->spkd", probs_low, grad_grouped, preferred_element_type=jnp.float32
    )
    centered = grad_probs - jnp.sum(grad_probs * probabilities, axis=-1, keepdims=True)
    grad_scores = (
        probabilities * centered * (1.0 - (capped / SOFT_CAP) ** 2) * query_scale()
    ).astype(jnp.bfloat16)
    query_rows_gradient = jnp.einsum(
        "skgqp,spkd->sqkgd", grad_scores, rotated_keys, preferred_element_type=jnp.float32
    ).reshape(seqs_here, length, q_heads, head_depth)
    key_rows_gradient = jnp.einsum(
        "skgqp,sqkgd->spkd", grad_scores, grouped_heads, preferred_element_type=jnp.float32
    )
    return (query_rows_gradient, key_rows_gradient, value_rows_gradient)


def normalize(hidden, pre_gain, pre_local):
    narrow = hidden.astype(jnp.float32)
    squares = one_axis_at_a_time(jnp.sum(narrow * narrow, axis=1), TENSOR)
    pre_scale = lax.rsqrt(squares[:, None] / pre_gain.shape[0] + NORM_EPS)
    normed = collect((narrow * pre_scale * pre_local).astype(jnp.bfloat16), TENSOR, 1)
    return (normed, pre_scale)


def attention_layer(hidden, normed, weights, adapters, lengths, post_local):
    w_query, w_key, value_projection, w_out, a_query, a_value = weights
    tok_rows, full_width = normed.shape
    seqs_here = lengths.shape[0]
    length = tok_rows // seqs_here
    query_rows = jnp.dot(normed, w_query, preferred_element_type=jnp.float32)
    keys_before_rotation = jnp.dot(normed, w_key, preferred_element_type=jnp.float32)
    value_rows = jnp.dot(normed, value_projection, preferred_element_type=jnp.float32)
    low_rank_update = None
    if adapters is not None:
        query_second_factor, value_second_factor = adapters
        rank_size = query_second_factor.shape[0]
        low_rank_update = jnp.dot(
            normed, jnp.concatenate([a_query, a_value], axis=1), preferred_element_type=jnp.float32
        ).astype(jnp.bfloat16)
        query_rows = query_rows + ADAPTER_SCALE * jnp.dot(
            low_rank_update[:, :rank_size], query_second_factor, preferred_element_type=jnp.float32
        )
        value_rows = value_rows + ADAPTER_SCALE * jnp.dot(
            low_rank_update[:, rank_size:], value_second_factor, preferred_element_type=jnp.float32
        )
    q_heads = query_rows.shape[1] // HEAD_SIZE
    kv_heads = keys_before_rotation.shape[1] // HEAD_SIZE
    query_rows = apply_rotation(
        query_rows.reshape(seqs_here, length, q_heads, HEAD_SIZE), 1.0
    ).astype(jnp.bfloat16)
    rotated_keys = apply_rotation(
        keys_before_rotation.reshape(seqs_here, length, kv_heads, HEAD_SIZE), 1.0
    ).astype(jnp.bfloat16)
    value_rows = value_rows.reshape(seqs_here, length, kv_heads, HEAD_SIZE).astype(jnp.bfloat16)
    mixed_out, probs_low, probabilities, capped = attend(
        query_rows, rotated_keys, value_rows, lengths
    )
    head_terms = lax.dot_general(
        mixed_out.reshape(tok_rows, q_heads * HEAD_SIZE),
        w_out,
        (((1,), (1,)), ((), ())),
        preferred_element_type=jnp.float32,
    )
    summed = summed_on_arrival(head_terms.astype(jnp.bfloat16), TENSOR, 1)
    squares = one_axis_at_a_time(jnp.sum(summed * summed, axis=1), TENSOR)
    post_scale = lax.rsqrt(squares[:, None] / full_width + NORM_EPS)
    result = hidden.astype(jnp.float32) + summed * post_scale * post_local
    saved = (
        low_rank_update,
        query_rows,
        rotated_keys,
        value_rows,
        probs_low,
        probabilities,
        capped,
        summed,
        post_scale,
    )
    return (result, saved)


def body(
    ref_hidden,
    pol_hidden,
    readout,
    lengths,
    pairing,
    pre_gain,
    post_gain,
    w_query,
    w_key,
    value_projection,
    w_out,
    a_query,
    a_value,
    query_second_factor,
    value_second_factor,
):
    tok_rows, part_width = pol_hidden.shape
    seqs_here = lengths.shape[0]
    length = tok_rows // seqs_here
    tensor_rank = lax.axis_index(TENSOR)
    data_rank = lax.axis_index(DP)
    all_seqs = seqs_here * lax.axis_size(DP)
    full_width = part_width * lax.axis_size(TENSOR)
    pre_local = lax.dynamic_slice_in_dim(pre_gain, tensor_rank * part_width, part_width)
    post_local = lax.dynamic_slice_in_dim(post_gain, tensor_rank * part_width, part_width)
    weights = sent_together((w_query, w_key, value_projection, w_out, a_query, a_value), DP, 0, 1)
    w_query_all, w_key_all, w_value_all, w_out_all, a_query_all, a_value_all = weights
    ref_normed, ref_scale = normalize(ref_hidden, pre_gain, pre_local)
    ref_result, ref_saved = attention_layer(
        ref_hidden, ref_normed, weights, None, lengths, post_local
    )
    pol_normed, pol_scale = normalize(pol_hidden, pre_gain, pre_local)
    pol_result, pol_saved = attention_layer(
        pol_hidden,
        pol_normed,
        weights,
        (query_second_factor, value_second_factor),
        lengths,
        post_local,
    )
    readout_wide = readout.astype(jnp.float32)
    living = (jnp.arange(length)[None, :] < lengths[:, None]).astype(jnp.float32)

    def sequence_score(result):
        return jnp.sum(
            jnp.sum(result * readout_wide, axis=1).reshape(seqs_here, length) * living, axis=1
        )

    placed = jnp.zeros((2, all_seqs), jnp.float32)
    offset = data_rank * seqs_here
    placed = lax.dynamic_update_slice(
        placed,
        jnp.stack([sequence_score(ref_result), sequence_score(pol_result)]),
        (jnp.int32(0), offset),
    )
    scores = one_axis_at_a_time(placed, DP_TENSOR)
    ratios = scores[1] - scores[0]
    chooser = (pairing[:, None] == jnp.arange(all_seqs)[None, :]).astype(jnp.float32)
    picked = jnp.dot(chooser, ratios, precision=lax.Precision.HIGHEST).reshape(-1, 2)
    margins = DPO_BETA * (picked[:, 0] - picked[:, 1])
    dpo_loss = jnp.sum(jax.nn.softplus(-margins))
    pair_pull = DPO_BETA * LOSS_SCALE * jax.nn.sigmoid(-margins)
    signed = jnp.stack([-pair_pull, pair_pull], axis=1).reshape(-1)
    coefficients = jnp.dot(signed, chooser, precision=lax.Precision.HIGHEST)
    local_coef = lax.dynamic_slice_in_dim(coefficients, offset, seqs_here)
    grad_result = (local_coef[:, None] * living).reshape(tok_rows, 1) * readout_wide
    (
        low_rank_update,
        query_rows,
        rotated_keys,
        value_rows,
        probs_low,
        probabilities,
        capped,
        summed,
        post_scale,
    ) = pol_saved
    post_dot = one_axis_at_a_time(jnp.sum(summed * post_local * grad_result, axis=1), TENSOR)
    grad_summed = (
        post_scale * post_local * grad_result
        - summed * post_scale**3 * post_dot[:, None] / full_width
    )
    grad_wide = collect(grad_summed.astype(jnp.bfloat16), TENSOR, 1)
    grad_mixed = jnp.dot(grad_wide, w_out_all, preferred_element_type=jnp.float32).astype(
        jnp.bfloat16
    )
    q_heads = query_rows.shape[2]
    grad_q_rot, rotated_key_gradient, value_head_gradient = attend_back(
        grad_mixed.reshape(seqs_here, length, q_heads, HEAD_SIZE),
        query_rows,
        rotated_keys,
        value_rows,
        probs_low,
        probabilities,
        capped,
    )
    query_rows_gradient = (
        apply_rotation(grad_q_rot, -1.0).reshape(tok_rows, -1).astype(jnp.bfloat16)
    )
    key_rows_gradient = (
        apply_rotation(rotated_key_gradient, -1.0).reshape(tok_rows, -1).astype(jnp.bfloat16)
    )
    value_rows_gradient = value_head_gradient.reshape(tok_rows, -1).astype(jnp.bfloat16)
    rank_size = query_second_factor.shape[0]
    rows_contraction = (((0,), (0,)), ((), ()))
    contract_cols = (((1,), (1,)), ((), ()))
    query_adapter_term = ADAPTER_SCALE * lax.dot_general(
        low_rank_update[:, :rank_size],
        query_rows_gradient,
        rows_contraction,
        preferred_element_type=jnp.float32,
    )
    value_adapter_term = ADAPTER_SCALE * lax.dot_general(
        low_rank_update[:, rank_size:],
        value_rows_gradient,
        rows_contraction,
        preferred_element_type=jnp.float32,
    )
    query_factor_gradient, value_factor_gradient = (
        over_copies(query_adapter_term.astype(jnp.bfloat16), DP).astype(jnp.float32),
        over_copies(value_adapter_term.astype(jnp.bfloat16), DP).astype(jnp.float32),
    )
    adapter_grad = jnp.concatenate(
        [
            ADAPTER_SCALE
            * lax.dot_general(
                query_rows_gradient,
                query_second_factor,
                contract_cols,
                preferred_element_type=jnp.float32,
            ),
            ADAPTER_SCALE
            * lax.dot_general(
                value_rows_gradient,
                value_second_factor,
                contract_cols,
                preferred_element_type=jnp.float32,
            ),
        ],
        axis=1,
    ).astype(jnp.bfloat16)
    adapter_term = lax.dot_general(
        pol_normed, adapter_grad, rows_contraction, preferred_element_type=jnp.float32
    )
    adapter_part = summed_on_arrival(adapter_term.astype(jnp.bfloat16), DP, 0)
    grad_a = lax.psum(adapter_part.astype(jnp.bfloat16), TENSOR).astype(jnp.float32)
    a_both = jnp.concatenate([a_query_all, a_value_all], axis=1)
    input_terms = lax.dot_general(
        query_rows_gradient, w_query_all, contract_cols, preferred_element_type=jnp.float32
    )
    input_terms = input_terms + lax.dot_general(
        key_rows_gradient, w_key_all, contract_cols, preferred_element_type=jnp.float32
    )
    input_terms = input_terms + lax.dot_general(
        value_rows_gradient, w_value_all, contract_cols, preferred_element_type=jnp.float32
    )
    input_terms = input_terms + lax.dot_general(
        adapter_grad, a_both, contract_cols, preferred_element_type=jnp.float32
    )
    input_whole = lax.psum(input_terms.astype(jnp.bfloat16), TENSOR).astype(jnp.float32)
    grad_normed = lax.dynamic_slice_in_dim(input_whole, tensor_rank * part_width, part_width, 1)
    narrow = pol_hidden.astype(jnp.float32)
    pre_dot = one_axis_at_a_time(jnp.sum(narrow * pre_local * grad_normed, axis=1), TENSOR)
    grad_hidden = (
        grad_result
        + pol_scale * pre_local * grad_normed
        - narrow * pol_scale**3 * pre_dot[:, None] / full_width
    )
    return (
        pol_result.astype(jnp.bfloat16),
        ref_result.astype(jnp.bfloat16),
        dpo_loss,
        grad_hidden.astype(jnp.bfloat16),
        grad_a,
        query_factor_gradient,
        value_factor_gradient,
    )


def solution(mesh):
    torus = Mesh(mesh.devices.reshape(4, 2, 4, 4), ("dp_0", "dp_1", "tensor_0", "tensor_1"))
    placed = (
        P(DP, TENSOR),
        P(DP, TENSOR),
        P(DP, TENSOR),
        P(DP),
        P(),
        P(),
        P(),
        P(DP, TENSOR),
        P(DP, TENSOR),
        P(DP, TENSOR),
        P(DP, TENSOR),
        P(DP, None),
        P(DP, None),
        P(None, TENSOR),
        P(None, TENSOR),
    )
    return jax.shard_map(
        body,
        mesh=torus,
        in_specs=placed,
        out_specs=(
            P(DP, TENSOR),
            P(DP, TENSOR),
            P(),
            P(DP, TENSOR),
            P(DP, None),
            P(None, TENSOR),
            P(None, TENSOR),
        ),
        check_vma=False,
    )
```

profile of v0, /device:TPU:0, one launch (start us, length us, event | category | flops | bytes accessed | tf_op | source)
XLA Modules:
  0.0 563.8 jit_solution(11571863054451459790)
XLA Ops:
  13.6 10.6 %all-reduce.3 = (f32[288]{0:T(512)S(1)}, f32[288]{0:T(512)S(1)}) all-reduce(f32[288]{0:T(512)S(1)} %get-tuple-element.60, f32[288]{0:T(512)S(1)} %get-tuple-element.59), channel_id=1, replica_groups=mesh['dp_0'=4,'dp_1'=2,'tensor_0'=4,'tensor_1'=4] {'tensor_0'}, use_global_device_ids=true, to_apply=%region_1.0 | all-reduce | flops 576 | bytes 4608 | tf_op jit(solution)/shard_map/psum | solution.py:23
  24.2 11.7 %all-reduce.1 = (f32[288]{0:T(512)S(1)}, f32[288]{0:T(512)S(1)}) all-reduce(f32[288]{0:T(512)S(1)} %get-tuple-element.17, f32[288]{0:T(512)S(1)} %get-tuple-element.18), channel_id=1, replica_groups=mesh['dp_0'=4,'dp_1'=2,'tensor_0'=4,'tensor_1'=4] {'tensor_1'}, use_global_device_ids=true, to_apply=%region_2.0 | all-reduce | flops 576 | bytes 4608 | tf_op jit(solution)/shard_map/psum | solution.py:23
  37.0 43.5 %all_to_all.40 = bf16[16,288,288]{2,1,0:T(8,128)(2,1)} all-to-all(bf16[16,288,288]{2,1,0:T(8,128)(2,1)S(1)} %broadcast_in_dim.31), channel_id=1, replica_groups=mesh['dp_0'=4,'dp_1'=2,'tensor_0'=4,'tensor_1'=4] {'tensor_0','tensor_1'}, dimensions={0} | all-to-all | bytes 5308416 | tf_op jit(solution)/shard_map/all_to_all | solution.py:28
  94.2 6.7 %dot_general.122 = bf16[3,96,4608]{2,1,0:T(8,128)(2,1)} reshape(bf16[288,16,288]{2,1,0:T(8,128)(2,1)} %copy.96) | data formatting | bytes 5308416 | tf_op jit(solution)/shard_map/dot_general | solution.py:161
  100.8 6.6 %reshape.391 = bf16[3,96,4608,1]{2,1,0,3:T(8,128)(2,1)} reshape(bf16[288,16,288]{2,1,0:T(8,128)(2,1)} %copy.96) | data formatting | bytes 5308416 | tf_op jit(solution)/shard_map/dot_general | solution.py:161
  107.5 21.0 %all-to-all-done = bf16[16,288,288]{2,1,0:T(8,128)(2,1)} async-done(((bf16[16,288,288]{2,1,0:T(8,128)(2,1)}), bf16[16,288,288]{2,1,0:T(8,128)(2,1)}, u32[]{:S(2)}, u32[]{:S(2)}) %all-to-all-start) | async-done | bytes 2654240 | tf_op jit(solution)/shard_map/all_to_all | solution.py:28
  139.1 7.2 %dot_general.114 = bf16[3,96,4608]{2,1,0:T(8,128)(2,1)} reshape(bf16[288,16,288]{2,1,0:T(8,128)(2,1)} %copy.87) | data formatting | bytes 5308416 | tf_op jit(solution)/shard_map/dot_general | solution.py:160
  188.9 9.0 %all-to-all-start.1 = ((bf16[16,288,288]{2,1,0:T(8,128)(2,1)}), bf16[16,288,288]{2,1,0:T(8,128)(2,1)}, u32[]{:S(2)}, u32[]{:S(2)}) async-start(bf16[16,288,288]{2,1,0:T(8,128)(2,1)} %bitcast.230), calls=%async_computation.1 | async-start | bytes 7077888 | tf_op jit(solution)/shard_map/all_to_all | solution.py:52
  216.0 25.3 %all-to-all-done.1 = bf16[16,288,288]{2,1,0:T(8,128)(2,1)} async-done(((bf16[16,288,288]{2,1,0:T(8,128)(2,1)}), bf16[16,288,288]{2,1,0:T(8,128)(2,1)}, u32[]{:S(2)}, u32[]{:S(2)}) %all-to-all-start.1) | async-done | bytes 2654240 | tf_op jit(solution)/shard_map/all_to_all | solution.py:52
  241.3 6.2 %all-to-all-start.3 = ((bf16[16,288,288]{2,1,0:T(8,128)(2,1)}), bf16[16,288,288]{2,1,0:T(8,128)(2,1)}, u32[]{:S(2)}, u32[]{:S(2)}) async-start(bf16[16,288,288]{2,1,0:T(8,128)(2,1)} %bitcast.229), calls=%async_computation.3 | async-start | bytes 7077888 | tf_op jit(solution)/shard_map/all_to_all | solution.py:52
  251.3 39.3 %all-to-all-done.3 = bf16[16,288,288]{2,1,0:T(8,128)(2,1)} async-done(((bf16[16,288,288]{2,1,0:T(8,128)(2,1)}), bf16[16,288,288]{2,1,0:T(8,128)(2,1)}, u32[]{:S(2)}, u32[]{:S(2)}) %all-to-all-start.3) | async-done | bytes 2654240 | tf_op jit(solution)/shard_map/all_to_all | solution.py:52
  293.4 9.2 %all-reduce.2 = (f32[288]{0:T(512)S(1)}, f32[288]{0:T(512)S(1)}) all-reduce(f32[288]{0:T(512)S(1)} %multiply_reduce_fusion.1, f32[288]{0:T(512)S(1)} %multiply_reduce_fusion), channel_id=1, replica_groups=mesh['dp_0'=4,'dp_1'=2,'tensor_0'=4,'tensor_1'=4] {'tensor_0'}, use_global_device_ids=true, to_apply=%region_6.7 | all-reduce | flops 576 | bytes 4608 | tf_op jit(solution)/shard_map/psum | solution.py:23
  302.6 9.1 %all-reduce = (f32[288]{0:T(512)S(1)}, f32[288]{0:T(512)S(1)}) all-reduce(f32[288]{0:T(512)S(1)} %get-tuple-element.15, f32[288]{0:T(512)S(1)} %get-tuple-element.16), channel_id=1, replica_groups=mesh['dp_0'=4,'dp_1'=2,'tensor_0'=4,'tensor_1'=4] {'tensor_1'}, use_global_device_ids=true, to_apply=%region_7.8 | all-reduce | flops 576 | bytes 4608 | tf_op jit(solution)/shard_map/psum | solution.py:23
  313.3 11.4 %psum.134 = f32[2,24]{1,0:T(2,128)S(1)} all-reduce(f32[2,24]{1,0:T(2,128)S(1)} %dynamic_update_slice.3), channel_id=1, replica_groups=mesh['dp_0'=4,'dp_1'=2,'tensor_0'=4,'tensor_1'=4] {'dp_0'}, use_global_device_ids=true, to_apply=%region_20.21 | all-reduce | flops 48 | bytes 384 | tf_op jit(solution)/shard_map/psum | solution.py:23
  327.2 8.9 %psum.136 = f32[2,24]{1,0:T(2,128)S(1)} all-reduce(f32[2,24]{1,0:T(2,128)S(1)} %psum.135), channel_id=1, replica_groups=mesh['dp_0'=4,'dp_1'=2,'tensor_0'=4,'tensor_1'=4] {'tensor_0'}, use_global_device_ids=true, to_apply=%region_22.23 | all-reduce | flops 48 | bytes 384 | tf_op jit(solution)/shard_map/psum | solution.py:23
  336.2 7.7 %psum.137 = f32[2,24]{1,0:T(2,128)S(1)} all-reduce(f32[2,24]{1,0:T(2,128)S(1)} %psum.136), channel_id=1, replica_groups=mesh['dp_0'=4,'dp_1'=2,'tensor_0'=4,'tensor_1'=4] {'tensor_1'}, use_global_device_ids=true, to_apply=%region_23.24 | all-reduce | flops 48 | bytes 384 | tf_op jit(solution)/shard_map/psum | solution.py:23
  345.0 8.5 %psum.138 = f32[288]{0:T(512)S(1)} all-reduce(f32[288]{0:T(512)S(1)} %fusion.63), channel_id=1, replica_groups=mesh['dp_0'=4,'dp_1'=2,'tensor_0'=4,'tensor_1'=4] {'tensor_0'}, use_global_device_ids=true, to_apply=%region_26.27 | all-reduce | flops 288 | bytes 2304 | tf_op jit(solution)/shard_map/psum | solution.py:23
  353.6 9.8 %psum.139 = f32[288]{0:T(512)S(1)} all-reduce(f32[288]{0:T(512)S(1)} %psum.138), channel_id=1, replica_groups=mesh['dp_0'=4,'dp_1'=2,'tensor_0'=4,'tensor_1'=4] {'tensor_1'}, use_global_device_ids=true, to_apply=%region_27.28 | all-reduce | flops 288 | bytes 2304 | tf_op jit(solution)/shard_map/psum | solution.py:23
  363.9 39.1 %all_to_all.41 = bf16[16,288,288]{2,1,0:T(8,128)(2,1)S(1)} all-to-all(bf16[16,288,288]{2,1,0:T(8,128)(2,1)S(1)} %broadcast_in_dim.33), channel_id=1, replica_groups=mesh['dp_0'=4,'dp_1'=2,'tensor_0'=4,'tensor_1'=4] {'tensor_0','tensor_1'}, dimensions={0} | all-to-all | bytes 5308416 | tf_op jit(solution)/shard_map/all_to_all | solution.py:28
  406.1 6.7 %reshape.378 = bf16[288,4608]{1,0:T(8,128)(2,1)} reshape(bf16[288,16,288]{2,1,0:T(8,128)(2,1)} %copy.103) | data formatting | bytes 5308416 | tf_op jit(solution)/shard_map/reshape | solution.py:36
  435.2 6.4 %all-to-all-done.5 = bf16[8,576,128]{2,1,0:T(8,128)(2,1)S(1)} async-done(((bf16[8,576,128]{2,1,0:T(8,128)(2,1)}), bf16[8,576,128]{2,1,0:T(8,128)(2,1)S(1)}, u32[]{:S(2)}, u32[]{:S(2)}) %all-to-all-start.5) | async-done | bytes 1179680 | tf_op jit(solution)/shard_map/all_to_all | solution.py:52
  465.1 68.0 %all-reduce.7.cloned.1.call-done = (bf16[288,4608]{1,0:T(8,128)(2,1)}, bf16[576,128]{1,0:T(8,128)(2,1)}) async-done(((bf16[288,4608]{1,0:T(8,128)(2,1)}, bf16[576,128]{1,0:T(8,128)(2,1)}), (bf16[288,4608]{1,0:T(8,128)(2,1)}, bf16[576,128]{1,0:T(8,128)(2,1)})) %all-reduce.7.cloned.1.call-update) | async-done | bytes 2801680 | tf_op jit(solution)/shard_map/psum | solution.py:371
  534.3 10.0 %psum.141 = f32[288]{0:T(512)S(1)} all-reduce(f32[288]{0:T(512)S(1)} %fusion.60), channel_id=1, replica_groups=mesh['dp_0'=4,'dp_1'=2,'tensor_0'=4,'tensor_1'=4] {'tensor_0'}, use_global_device_ids=true, to_apply=%region_31.32 | all-reduce | flops 288 | bytes 2304 | tf_op jit(solution)/shard_map/psum | solution.py:23
  544.3 8.8 %psum.142 = f32[288]{0:T(512)S(1)} all-reduce(f32[288]{0:T(512)S(1)} %psum.141), channel_id=1, replica_groups=mesh['dp_0'=4,'dp_1'=2,'tensor_0'=4,'tensor_1'=4] {'tensor_1'}, use_global_device_ids=true, to_apply=%region_32.33 | all-reduce | flops 288 | bytes 2304 | tf_op jit(solution)/shard_map/psum | solution.py:23
  (187 shorter events, 157.9 us)
Async XLA Ops:
  7.2 152.7 %copy-start = (bf16[64,256]{1,0:T(8,128)(2,1)S(1)}, bf16[64,256]{1,0:T(8,128)(2,1)}, u32[]{:S(2)}) copy-start(bf16[64,256]{1,0:T(8,128)(2,1)} %param.28) | copy-start | bytes 98308
  7.2 6.2 %copy-start.3 = (bf16[288,288]{1,0:T(8,128)(2,1)S(1)}, bf16[288,288]{1,0:T(8,128)(2,1)}, u32[]{:S(2)}) copy-start(bf16[288,288]{1,0:T(8,128)(2,1)} %param.16) | copy-start | bytes 497668
  7.2 6.2 %copy-start.8 = (bf16[288,288]{1,0:T(8,128)(2,1)S(1)}, bf16[288,288]{1,0:T(8,128)(2,1)}, u32[]{:S(2)}) copy-start(bf16[288,288]{1,0:T(8,128)(2,1)} %param.15) | copy-start | bytes 497668
  7.2 139.1 %all-gather.2.cloned.1.call-start = ((), (), s32[]{:S(2)}) async-start(), calls=%async_computation.8 | async-start | bytes 9289728 | tf_op jit(solution)/shard_map/all_gather | solution.py:62
  82.7 4.7 copy-start.31
  82.7 45.8 %all-to-all-start = ((bf16[16,288,288]{2,1,0:T(8,128)(2,1)}), bf16[16,288,288]{2,1,0:T(8,128)(2,1)}, u32[]{:S(2)}, u32[]{:S(2)}) async-start(bf16[16,288,288]{2,1,0:T(8,128)(2,1)} %broadcast_in_dim.24), calls=%async_computation | async-start | bytes 7077888 | tf_op jit(solution)/shard_map/all_to_all | solution.py:28
  139.1 33.9 %copy-start.1 = (bf16[288,4608]{1,0:T(8,128)(2,1)}, bf16[288,4608]{1,0:T(8,128)(2,1)S(1)}, u32[]{:S(2)}) copy-start(bf16[288,4608]{1,0:T(8,128)(2,1)S(1)} %reshape.369) | copy-start | bytes 7962628
  162.2 3.5 copy-start.5
  188.9 9.0 %copy-start.21 = (bf16[3,96,2,64]{3,1,2,0:T(8,128)(2,1)S(1)}, bf16[3,96,2,64]{3,1,2,0:T(8,128)(2,1)}, u32[]{:S(2)}) copy-start(bf16[3,96,2,64]{3,1,2,0:T(8,128)(2,1)} %get-tuple-element.30) | copy-start | bytes 221188
  188.9 9.0 %copy-start.22 = (bf16[3,96,2,64]{3,1,2,0:T(8,128)(2,1)S(1)}, bf16[3,96,2,64]{3,1,2,0:T(8,128)(2,1)}, u32[]{:S(2)}) copy-start(bf16[3,96,2,64]{3,1,2,0:T(8,128)(2,1)} %get-tuple-element.31) | copy-start | bytes 221188
  188.9 11.6 %copy-start.6 = (bf16[3,96,4608]{2,1,0:T(8,128)(2,1)S(1)}, bf16[3,96,4608]{2,1,0:T(8,128)(2,1)}, u32[]{:S(2)}) copy-start(bf16[3,96,4608]{2,1,0:T(8,128)(2,1)} %dot_general.122) | copy-start | bytes 7962628
  188.9 52.4 %all-to-all-start.1 = ((bf16[16,288,288]{2,1,0:T(8,128)(2,1)}), bf16[16,288,288]{2,1,0:T(8,128)(2,1)}, u32[]{:S(2)}, u32[]{:S(2)}) async-start(bf16[16,288,288]{2,1,0:T(8,128)(2,1)} %bitcast.230), calls=%async_computation.1 | async-start | bytes 7077888 | tf_op jit(solution)/shard_map/all_to_all | solution.py:52
  241.3 7.0 %copy-start.33 = (s32[24]{0:T(128)S(1)}, s32[24]{0:T(128)}, u32[]{:S(2)}) copy-start(s32[24]{0:T(128)} %param.19) | copy-start | bytes 292
  241.3 49.3 %all-to-all-start.3 = ((bf16[16,288,288]{2,1,0:T(8,128)(2,1)}), bf16[16,288,288]{2,1,0:T(8,128)(2,1)}, u32[]{:S(2)}, u32[]{:S(2)}) async-start(bf16[16,288,288]{2,1,0:T(8,128)(2,1)} %bitcast.229), calls=%async_computation.3 | async-start | bytes 7077888 | tf_op jit(solution)/shard_map/all_to_all | solution.py:52
  251.1 60.5 %copy-start.4 = (bf16[288,288]{1,0:T(8,128)(2,1)S(1)}, bf16[288,288]{1,0:T(8,128)(2,1)}, u32[]{:S(2)}) copy-start(bf16[288,288]{1,0:T(8,128)(2,1)} %param.17) | copy-start | bytes 497668
  251.3 61.6 %copy-start.32 = (s32[3]{0:T(128)S(1)}, s32[3]{0:T(128)}, u32[]{:S(2)}) copy-start(s32[3]{0:T(128)} %param.18) | copy-start | bytes 40
  412.7 3.5 copy-start.24
  412.7 3.5 copy-start.30
  412.7 3.8 copy-start.35
  420.8 20.8 %all-to-all-start.5 = ((bf16[8,576,128]{2,1,0:T(8,128)(2,1)}), bf16[8,576,128]{2,1,0:T(8,128)(2,1)S(1)}, u32[]{:S(2)}, u32[]{:S(2)}) async-start(bf16[8,576,128]{2,1,0:T(8,128)(2,1)} %bitcast.71), calls=%async_computation.5 | async-start | bytes 2359296 | tf_op jit(solution)/shard_map/all_to_all | solution.py:52
  424.4 108.7 %all-reduce.7.cloned.1.call-start = ((), (), s32[]{:S(2)}) async-start(), calls=%async_computation.9 | async-start | bytes 5603328 | tf_op jit(solution)/shard_map/psum | solution.py:371
  442.5 112.2 %copy-start.28 = (f32[288]{0:T(512)S(1)}, f32[288]{0:T(512)}, u32[]{:S(2)}) copy-start(f32[288]{0:T(512)} %get-tuple-element.44) | copy-start | bytes 3460
  443.5 9.4 %all-to-all-start.7 = ((bf16[8,64,128]{2,1,0:T(8,128)(2,1)}), bf16[8,64,128]{2,1,0:T(8,128)(2,1)S(1)}, u32[]{:S(2)}, u32[]{:S(2)}) async-start(bf16[8,64,128]{2,1,0:T(8,128)(2,1)} %broadcast_in_dim.35), calls=%async_computation.7 | async-start | bytes 262144 | tf_op jit(solution)/shard_map/all_to_all | solution.py:28
  453.6 10.9 %all-to-all-start.6 = ((bf16[8,64,256]{2,1,0:T(8,128)(2,1)}), bf16[8,64,256]{2,1,0:T(8,128)(2,1)S(1)}, u32[]{:S(2)}, u32[]{:S(2)}) async-start(bf16[8,64,256]{2,1,0:T(8,128)(2,1)} %broadcast_in_dim.34), calls=%async_computation.6 | async-start | bytes 524288 | tf_op jit(solution)/shard_map/all_to_all | solution.py:28
  (20 other events, 32.9 us)
Sparse Core Ops, SparseCore 0:
  12.7 51.5 all-gather.1
  442.6 90.4 all-reduce.6
where the time goes:
time: 573 us; the launch traced here: 564 us
  blocking collectives  191 us (33%)
  waiting for transfers between devices  172 us (30%)
  local copies, waits for them, and re-layouts  89.7 us (16%)
  matrix products  45.7 us (8%)
  starting transfers between devices  30.3 us (5%)
  other arithmetic  20.1 us (4%)
  between operations  15 us (3%)
    psum x12, blocking collectives, one_axis_at_a_time(): return functools.reduce(lax.psum, axes, shard)  108 us
    all_to_all x2, blocking collectives, copy_for_each(): lax.all_to_all(jnp.broadcast_to(shard[None], (count, *shard.shape)), axis...  82.7 us
    all_to_all x3, waiting for transfers between devices, summed_on_arrival(): lax.all_to_all(tiles, axis, split_axis=0, concat_axis=0, tiled=True)  71.1 us
    psum x1, waiting for transfers between devices, body(): lax.psum(input_terms.astype(jnp.bfloat16), TENSOR).astype(jnp.float32)  68 us
    all_to_all x3, waiting for transfers between devices, copy_for_each(): lax.all_to_all(jnp.broadcast_to(shard[None], (count, *shard.shape)), axis...  33 us
    reshape x4, local copies, waits for them, and re-layouts, split_up(): shard.reshape(*shape[:dim], count, shape[dim] // count, *shape[dim + 1:])  20.9 us
    all_to_all x3, starting transfers between devices, summed_on_arrival(): lax.all_to_all(tiles, axis, split_axis=0, concat_axis=0, tiled=True)  18.8 us
    dot_general x2, local copies, waits for them, and re-layouts, attention_layer(): jnp.dot(normed, value_projection, preferred_element_type=jnp.float32)  13.3 us
  transfers between devices with their start and end apart: 8, of which 7 were waited for; matrix products, arithmetic and copies ran while one was open for 14% of the time, Pallas kernels for 0%

commit v1 on v0

--- a/solution.py
+++ b/solution.py
@@ -17,6 +17,14 @@
 DPO_BETA = 0.5
 LOSS_SCALE = 256.0
 ROPE_BASE = 10000.0
+
+
+def feed_the_local_data(original, axis_tag):
+    b_next = jnp.sum(lax.all_gather(original, axis_tag), axis=0)
+    return b_next
+
+
+values_number = functools.partial(feed_the_local_data, axis_tag=TENSOR)
 
 
 def one_axis_at_a_time(shard, axes):
@@ -368,7 +376,7 @@
     input_terms = input_terms + lax.dot_general(
         adapter_grad, a_both, contract_cols, preferred_element_type=jnp.float32
     )
-    input_whole = lax.psum(input_terms.astype(jnp.bfloat16), TENSOR).astype(jnp.float32)
+    input_whole = values_number(input_terms.astype(jnp.bfloat16)).astype(jnp.float32)
     grad_normed = lax.dynamic_slice_in_dim(input_whole, tensor_rank * part_width, part_width, 1)
     narrow = pol_hidden.astype(jnp.float32)
     pre_dot = one_axis_at_a_time(jnp.sum(narrow * pre_local * grad_normed, axis=1), TENSOR)

time: 573 us -> 820 us (1.43)
  waiting for transfers between devices: 172 us -> 400 us
  other arithmetic: 20.1 us -> 33 us
    all_gather x0 -> x1, waiting for transfers between devices: none -> 242 us  [feed_the_local_data(): b_next = jnp.sum(lax.all_gather(original, axis_tag), axis=0)]
    psum x1, waiting for transfers between devices: 68 us -> 52.8 us  [body(): lax.psum(adapter_part.astype(jnp.bfloat16), TENSOR).astype(jnp.float32)]
    reduce_sum x0 -> x1, other arithmetic: none -> 14.3 us  [feed_the_local_data(): b_next = jnp.sum(lax.all_gather(original, axis_tag), axis=0)]
  transfers between devices with their start and end apart: 8 -> 9, of which waited for: 7 -> 8; matrix products, arithmetic and copies ran while one was open for 14% -> 10% of each run, Pallas kernels for 0% -> 0%
where the time goes in v1:
time: 820 us; the launch traced here: 811 us
  waiting for transfers between devices  400 us (49%)
  blocking collectives  191 us (23%)
  local copies, waits for them, and re-layouts  89.8 us (11%)
  matrix products  51.4 us (6%)
  other arithmetic  33 us (4%)
  starting transfers between devices  30.4 us (4%)
  between operations  14.7 us (2%)
    all_gather x1, waiting for transfers between devices, feed_the_local_data(): b_next = jnp.sum(lax.all_gather(original, axis_tag), axis=0)  242 us
    psum x12, blocking collectives, one_axis_at_a_time(): return functools.reduce(lax.psum, axes, shard)  108 us
    all_to_all x2, blocking collectives, copy_for_each(): lax.all_to_all(jnp.broadcast_to(shard[None], (count, *shard.shape)), axis...  82.6 us
    all_to_all x3, waiting for transfers between devices, summed_on_arrival(): lax.all_to_all(tiles, axis, split_axis=0, concat_axis=0, tiled=True)  72.4 us
    psum x1, waiting for transfers between devices, body(): lax.psum(adapter_part.astype(jnp.bfloat16), TENSOR).astype(jnp.float32)  52.8 us
    all_to_all x3, waiting for transfers between devices, copy_for_each(): lax.all_to_all(jnp.broadcast_to(shard[None], (count, *shard.shape)), axis...  33.1 us
    reshape x4, local copies, waits for them, and re-layouts, split_up(): shard.reshape(*shape[:dim], count, shape[dim] // count, *shape[dim + 1:])  21 us
    all_to_all x3, starting transfers between devices, summed_on_arrival(): lax.all_to_all(tiles, axis, split_axis=0, concat_axis=0, tiled=True)  18.8 us
  transfers between devices with their start and end apart: 9, of which 8 were waited for; matrix products, arithmetic and copies ran while one was open for 10% of the time, Pallas kernels for 0%

profile of v1, /device:TPU:0, one launch (start us, length us, event | category | flops | bytes accessed | tf_op | source)
XLA Modules:
  0.0 810.8 jit_solution(10329011098672244443)
XLA Ops:
  13.6 10.6 %all-reduce.3 = (f32[288]{0:T(512)S(1)}, f32[288]{0:T(512)S(1)}) all-reduce(f32[288]{0:T(512)S(1)} %get-tuple-element.58, f32[288]{0:T(512)S(1)} %get-tuple-element.57), channel_id=1, replica_groups=mesh['dp_0'=4,'dp_1'=2,'tensor_0'=4,'tensor_1'=4] {'tensor_0'}, use_global_device_ids=true, to_apply=%region_1.0 | all-reduce | flops 576 | bytes 4608 | tf_op jit(solution)/shard_map/psum | solution.py:31
  24.2 11.7 %all-reduce.1 = (f32[288]{0:T(512)S(1)}, f32[288]{0:T(512)S(1)}) all-reduce(f32[288]{0:T(512)S(1)} %get-tuple-element.17, f32[288]{0:T(512)S(1)} %get-tuple-element.18), channel_id=1, replica_groups=mesh['dp_0'=4,'dp_1'=2,'tensor_0'=4,'tensor_1'=4] {'tensor_1'}, use_global_device_ids=true, to_apply=%region_2.0 | all-reduce | flops 576 | bytes 4608 | tf_op jit(solution)/shard_map/psum | solution.py:31
  37.1 43.5 %all_to_all.40 = bf16[16,288,288]{2,1,0:T(8,128)(2,1)} all-to-all(bf16[16,288,288]{2,1,0:T(8,128)(2,1)S(1)} %broadcast_in_dim.31), channel_id=1, replica_groups=mesh['dp_0'=4,'dp_1'=2,'tensor_0'=4,'tensor_1'=4] {'tensor_0','tensor_1'}, dimensions={0} | all-to-all | bytes 5308416 | tf_op jit(solution)/shard_map/all_to_all | solution.py:36
  94.2 6.6 dot_general.122
  100.8 6.6 reshape.392
  107.5 21.1 %all-to-all-done = bf16[16,288,288]{2,1,0:T(8,128)(2,1)} async-done(((bf16[16,288,288]{2,1,0:T(8,128)(2,1)}), bf16[16,288,288]{2,1,0:T(8,128)(2,1)}, u32[]{:S(2)}, u32[]{:S(2)}) %all-to-all-start) | async-done | bytes 2654240 | tf_op jit(solution)/shard_map/all_to_all | solution.py:36
  139.3 7.2 dot_general.114
  189.2 9.0 %all-to-all-start.1 = ((bf16[16,288,288]{2,1,0:T(8,128)(2,1)}), bf16[16,288,288]{2,1,0:T(8,128)(2,1)}, u32[]{:S(2)}, u32[]{:S(2)}) async-start(bf16[16,288,288]{2,1,0:T(8,128)(2,1)} %bitcast.232), calls=%async_computation.1 | async-start | bytes 7077888 | tf_op jit(solution)/shard_map/all_to_all | solution.py:60
  216.3 25.3 %all-to-all-done.1 = bf16[16,288,288]{2,1,0:T(8,128)(2,1)} async-done(((bf16[16,288,288]{2,1,0:T(8,128)(2,1)}), bf16[16,288,288]{2,1,0:T(8,128)(2,1)}, u32[]{:S(2)}, u32[]{:S(2)}) %all-to-all-start.1) | async-done | bytes 2654240 | tf_op jit(solution)/shard_map/all_to_all | solution.py:60
  251.6 39.3 %all-to-all-done.3 = bf16[16,288,288]{2,1,0:T(8,128)(2,1)} async-done(((bf16[16,288,288]{2,1,0:T(8,128)(2,1)}), bf16[16,288,288]{2,1,0:T(8,128)(2,1)}, u32[]{:S(2)}, u32[]{:S(2)}) %all-to-all-start.3) | async-done | bytes 2654240 | tf_op jit(solution)/shard_map/all_to_all | solution.py:60
  293.7 9.2 %all-reduce.2 = (f32[288]{0:T(512)S(1)}, f32[288]{0:T(512)S(1)}) all-reduce(f32[288]{0:T(512)S(1)} %multiply_reduce_fusion.1, f32[288]{0:T(512)S(1)} %multiply_reduce_fusion), channel_id=1, replica_groups=mesh['dp_0'=4,'dp_1'=2,'tensor_0'=4,'tensor_1'=4] {'tensor_0'}, use_global_device_ids=true, to_apply=%region_6.7 | all-reduce | flops 576 | bytes 4608 | tf_op jit(solution)/shard_map/psum | solution.py:31
  302.8 9.1 %all-reduce = (f32[288]{0:T(512)S(1)}, f32[288]{0:T(512)S(1)}) all-reduce(f32[288]{0:T(512)S(1)} %get-tuple-element.15, f32[288]{0:T(512)S(1)} %get-tuple-element.16), channel_id=1, replica_groups=mesh['dp_0'=4,'dp_1'=2,'tensor_0'=4,'tensor_1'=4] {'tensor_1'}, use_global_device_ids=true, to_apply=%region_7.8 | all-reduce | flops 576 | bytes 4608 | tf_op jit(solution)/shard_map/psum | solution.py:31
  313.6 11.4 %psum.127 = f32[2,24]{1,0:T(2,128)S(1)} all-reduce(f32[2,24]{1,0:T(2,128)S(1)} %dynamic_update_slice.3), channel_id=1, replica_groups=mesh['dp_0'=4,'dp_1'=2,'tensor_0'=4,'tensor_1'=4] {'dp_0'}, use_global_device_ids=true, to_apply=%region_20.21 | all-reduce | flops 48 | bytes 384 | tf_op jit(solution)/shard_map/psum | solution.py:31
  327.5 8.7 %psum.129 = f32[2,24]{1,0:T(2,128)S(1)} all-reduce(f32[2,24]{1,0:T(2,128)S(1)} %psum.128), channel_id=1, replica_groups=mesh['dp_0'=4,'dp_1'=2,'tensor_0'=4,'tensor_1'=4] {'tensor_0'}, use_global_device_ids=true, to_apply=%region_22.23 | all-reduce | flops 48 | bytes 384 | tf_op jit(solution)/shard_map/psum | solution.py:31
  336.1 7.7 psum.130
  345.5 8.8 %psum.131 = f32[288]{0:T(512)S(1)} all-reduce(f32[288]{0:T(512)S(1)} %fusion.63), channel_id=1, replica_groups=mesh['dp_0'=4,'dp_1'=2,'tensor_0'=4,'tensor_1'=4] {'tensor_0'}, use_global_device_ids=true, to_apply=%region_26.27 | all-reduce | flops 288 | bytes 2304 | tf_op jit(solution)/shard_map/psum | solution.py:31
  354.3 9.8 %psum.132 = f32[288]{0:T(512)S(1)} all-reduce(f32[288]{0:T(512)S(1)} %psum.131), channel_id=1, replica_groups=mesh['dp_0'=4,'dp_1'=2,'tensor_0'=4,'tensor_1'=4] {'tensor_1'}, use_global_device_ids=true, to_apply=%region_27.28 | all-reduce | flops 288 | bytes 2304 | tf_op jit(solution)/shard_map/psum | solution.py:31
  364.6 39.1 %all_to_all.41 = bf16[16,288,288]{2,1,0:T(8,128)(2,1)S(1)} all-to-all(bf16[16,288,288]{2,1,0:T(8,128)(2,1)S(1)} %broadcast_in_dim.33), channel_id=1, replica_groups=mesh['dp_0'=4,'dp_1'=2,'tensor_0'=4,'tensor_1'=4] {'tensor_0','tensor_1'}, dimensions={0} | all-to-all | bytes 5308416 | tf_op jit(solution)/shard_map/all_to_all | solution.py:36
  436.3 7.8 all-to-all-done.5
  472.9 52.8 %all-reduce.6.cloned.1.call-done = bf16[576,128]{1,0:T(8,128)(2,1)} async-done(((bf16[576,128]{1,0:T(8,128)(2,1)}), bf16[576,128]{1,0:T(8,128)(2,1)}) %all-reduce.6.cloned.1.call-update) | async-done | bytes 147472 | tf_op jit(solution)/shard_map/psum | solution.py:365
  527.4 242.0 %all-gather.6.cloned.1.call-done = bf16[4608,4608]{1,0:T(8,128)(2,1)} async-done(((bf16[288,4608]{1,0:T(8,128)(2,1)}), bf16[4608,4608]{1,0:T(8,128)(2,1)}) %all-gather.6.cloned.1.call-update) | async-done | bytes 42467344 | tf_op jit(solution)/shard_map/all_gather | solution.py:23
  769.4 14.3 %reduce_sum.201 = bf16[288,4608]{1,0:T(8,128)(2,1)S(1)} reduce(bf16[16,288,4608]{2,1,0:T(8,128)(2,1)} %bitcast.230, bf16[]{:T(256)} %constant.84.clone.1), dimensions={0}, to_apply=%region_29.30 | reduce | flops 19906560 | bytes 45121536 | tf_op jit(solution)/shard_map/reduce_sum | solution.py:23
  784.0 10.4 %psum.133 = f32[288]{0:T(512)S(1)} all-reduce(f32[288]{0:T(512)S(1)} %fusion.60), channel_id=1, replica_groups=mesh['dp_0'=4,'dp_1'=2,'tensor_0'=4,'tensor_1'=4] {'tensor_0'}, use_global_device_ids=true, to_apply=%region_31.32 | all-reduce | flops 288 | bytes 2304 | tf_op jit(solution)/shard_map/psum | solution.py:31
  794.4 8.6 %psum.134 = f32[288]{0:T(512)S(1)} all-reduce(f32[288]{0:T(512)S(1)} %psum.133), channel_id=1, replica_groups=mesh['dp_0'=4,'dp_1'=2,'tensor_0'=4,'tensor_1'=4] {'tensor_1'}, use_global_device_ids=true, to_apply=%region_32.33 | all-reduce | flops 288 | bytes 2304 | tf_op jit(solution)/shard_map/psum | solution.py:31
  (193 shorter events, 175.4 us)
Async XLA Ops:
  7.2 152.8 %copy-start = (bf16[64,256]{1,0:T(8,128)(2,1)S(1)}, bf16[64,256]{1,0:T(8,128)(2,1)}, u32[]{:S(2)}) copy-start(bf16[64,256]{1,0:T(8,128)(2,1)} %param.28) | copy-start | bytes 98308
  7.2 6.2 copy-start.3
  7.2 6.2 copy-start.8
  7.2 139.3 %all-gather.4.cloned.1.call-start = ((), (), s32[]{:S(2)}) async-start(), calls=%async_computation.8 | async-start | bytes 9289728 | tf_op jit(solution)/shard_map/all_gather | solution.py:70
  36.6 44.0 %copy-start.28 = (f32[288]{0:T(512)}, f32[288]{0:T(512)S(1)}, u32[]{:S(2)}) copy-start(f32[288]{0:T(512)S(1)} %get-tuple-element.43) | copy-start | bytes 3460
  82.7 4.7 copy-start.33
  82.7 45.8 %all-to-all-start = ((bf16[16,288,288]{2,1,0:T(8,128)(2,1)}), bf16[16,288,288]{2,1,0:T(8,128)(2,1)}, u32[]{:S(2)}, u32[]{:S(2)}) async-start(bf16[16,288,288]{2,1,0:T(8,128)(2,1)} %broadcast_in_dim.24), calls=%async_computation | async-start | bytes 7077888 | tf_op jit(solution)/shard_map/all_to_all | solution.py:36
  139.3 33.9 %copy-start.1 = (bf16[288,4608]{1,0:T(8,128)(2,1)}, bf16[288,4608]{1,0:T(8,128)(2,1)S(1)}, u32[]{:S(2)}) copy-start(bf16[288,4608]{1,0:T(8,128)(2,1)S(1)} %reshape.369) | copy-start | bytes 7962628
  189.2 9.0 %copy-start.21 = (bf16[3,96,2,64]{3,1,2,0:T(8,128)(2,1)S(1)}, bf16[3,96,2,64]{3,1,2,0:T(8,128)(2,1)}, u32[]{:S(2)}) copy-start(bf16[3,96,2,64]{3,1,2,0:T(8,128)(2,1)} %get-tuple-element.28) | copy-start | bytes 221188
  189.2 9.0 %copy-start.22 = (bf16[3,96,2,64]{3,1,2,0:T(8,128)(2,1)S(1)}, bf16[3,96,2,64]{3,1,2,0:T(8,128)(2,1)}, u32[]{:S(2)}) copy-start(bf16[3,96,2,64]{3,1,2,0:T(8,128)(2,1)} %get-tuple-element.29) | copy-start | bytes 221188
  189.2 11.6 %copy-start.6 = (bf16[3,96,4608]{2,1,0:T(8,128)(2,1)S(1)}, bf16[3,96,4608]{2,1,0:T(8,128)(2,1)}, u32[]{:S(2)}) copy-start(bf16[3,96,4608]{2,1,0:T(8,128)(2,1)} %dot_general.122) | copy-start | bytes 7962628
  189.2 52.4 %all-to-all-start.1 = ((bf16[16,288,288]{2,1,0:T(8,128)(2,1)}), bf16[16,288,288]{2,1,0:T(8,128)(2,1)}, u32[]{:S(2)}, u32[]{:S(2)}) async-start(bf16[16,288,288]{2,1,0:T(8,128)(2,1)} %bitcast.232), calls=%async_computation.1 | async-start | bytes 7077888 | tf_op jit(solution)/shard_map/all_to_all | solution.py:60
  241.6 7.0 copy-start.34
  241.6 49.3 %all-to-all-start.3 = ((bf16[16,288,288]{2,1,0:T(8,128)(2,1)}), bf16[16,288,288]{2,1,0:T(8,128)(2,1)}, u32[]{:S(2)}, u32[]{:S(2)}) async-start(bf16[16,288,288]{2,1,0:T(8,128)(2,1)} %bitcast.231), calls=%async_computation.3 | async-start | bytes 7077888 | tf_op jit(solution)/shard_map/all_to_all | solution.py:60
  251.5 60.5 %copy-start.4 = (bf16[288,288]{1,0:T(8,128)(2,1)S(1)}, bf16[288,288]{1,0:T(8,128)(2,1)}, u32[]{:S(2)}) copy-start(bf16[288,288]{1,0:T(8,128)(2,1)} %param.17) | copy-start | bytes 497668
  415.7 4.1 copy-start.18
  423.3 20.8 %all-to-all-start.5 = ((bf16[8,576,128]{2,1,0:T(8,128)(2,1)}), bf16[8,576,128]{2,1,0:T(8,128)(2,1)S(1)}, u32[]{:S(2)}, u32[]{:S(2)}) async-start(bf16[8,576,128]{2,1,0:T(8,128)(2,1)} %bitcast.72), calls=%async_computation.5 | async-start | bytes 2359296 | tf_op jit(solution)/shard_map/all_to_all | solution.py:60
  426.8 98.9 %all-reduce.6.cloned.1.call-start = ((), (), s32[]{:S(2)}) async-start(), calls=%async_computation.9 | async-start | bytes 294912 | tf_op jit(solution)/shard_map/psum | solution.py:365
  445.0 324.4 %all-gather.6.cloned.1.call-start = ((), (), s32[]{:S(2)}) async-start(), calls=%async_computation.10 | async-start | bytes 45121536 | tf_op jit(solution)/shard_map/all_gather | solution.py:23
  450.3 14.5 %copy-start.35 = (f32[12,1]{0,1:T(1,128)S(1)}, f32[12,1]{0,1:T(1,128)}, u32[]{:S(2)}) copy-start(f32[12,1]{0,1:T(1,128)} %get-tuple-element.21) | copy-start | bytes 148
  451.3 9.4 %all-to-all-start.7 = ((bf16[8,64,128]{2,1,0:T(8,128)(2,1)}), bf16[8,64,128]{2,1,0:T(8,128)(2,1)S(1)}, u32[]{:S(2)}, u32[]{:S(2)}) async-start(bf16[8,64,128]{2,1,0:T(8,128)(2,1)} %broadcast_in_dim.35), calls=%async_computation.7 | async-start | bytes 262144 | tf_op jit(solution)/shard_map/all_to_all | solution.py:36
  461.4 10.9 %all-to-all-start.6 = ((bf16[8,64,256]{2,1,0:T(8,128)(2,1)}), bf16[8,64,256]{2,1,0:T(8,128)(2,1)S(1)}, u32[]{:S(2)}, u32[]{:S(2)}) async-start(bf16[8,64,256]{2,1,0:T(8,128)(2,1)} %broadcast_in_dim.34), calls=%async_computation.6 | async-start | bytes 524288 | tf_op jit(solution)/shard_map/all_to_all | solution.py:36
  769.4 33.6 %copy-start.29 = (f32[288]{0:T(512)S(1)}, f32[288]{0:T(512)}, u32[]{:S(2)}) copy-start(f32[288]{0:T(512)} %copy-done.28) | copy-start | bytes 3460
  769.4 33.6 %copy-start.30 = (f32[288]{0:T(512)S(1)}, f32[288]{0:T(512)}, u32[]{:S(2)}) copy-start(f32[288]{0:T(512)} %get-tuple-element.42) | copy-start | bytes 3460
  (22 other events, 55.1 us)
Sparse Core Ops, SparseCore 0:
  12.7 51.5 all-gather.3
  445.1 80.6 all-reduce.5
  528.0 241.3 all-gather.5
